TPU v7x, 32 devices: a whole 2x2x4 slice. The times are simulated.
32 devices in a mesh: groups: 2 (over y), wide: 4 (over z), narrow: 4 (over x, core).
Axes of the slice: x: 2, y: 2, z: 4, core: 2. Of those that a mesh axis runs over, the one named last changes fastest.
Arguments:
- cont_queries: bfloat16 [32, 128, 64, 128], P(('groups', 'wide'), None, 'narrow'), parts along dimension 0, may hold values from -5 to 5
- cont_keys: bfloat16 [32, 128, 8, 128], P(('groups', 'wide'), None, 'narrow'), parts along dimension 0, may hold values from -5 to 5
- cont_values: bfloat16 [32, 128, 8, 128], P(('groups', 'wide'), None, 'narrow'), parts along dimension 0, may hold values from -5 to 5
- prefix_kv: bfloat16 [8, 2, 128, 8, 128], P(('groups', 'wide'), None, None, 'narrow'), parts along dimension 0, may hold values from -5 to 5
- probe: bfloat16 [64, 128], P('narrow'), may hold values from -0.5 to 0.5
- question_row: int32 [8], P('groups'), parts along dimension 0, may hold values from 0 to 3, each once
- cont_slot: int32 [32], P(('groups', 'wide')), parts along dimension 0, may hold values from 0 to 15, each once
- cont_length: int32 [32], P(('groups', 'wide')), parts along dimension 0, may hold values from 1 to 128
- gold: int32 [8], P('groups'), parts along dimension 0, may hold values from 0 to 3
Outputs:
- token_score: float32 [32, 128], P(('groups', 'wide')), parts along dimension 0
- owned_logprob: float32 [8, 4], P(('groups', 'wide')), parts along dimension 0
- owned_loss: float32 [8], P(('groups', 'wide')), parts along dimension 0
There are 2 independent parts, one for each index of `groups`. A program takes and returns all parts, laid end to end along the dimension named above; an argument that names none is the same for every part. Nothing has to cross between parts.
All inputs are finite; a program needn't handle non-finite values.
Results may differ from a plain program's by a relative error of at most 0.0065.
Values may be sent and summed in bfloat16 or wider, within the bound.
No kernel may reach another device: no remote copies, remote signals or barrier semaphores. Data moves between devices by JAX's collectives and lax.ppermute only.
A program may use at most 64 MiB of HBM per device.

v0:
```python
import jax
import jax.numpy as jnp
from jax import lax
from jax.sharding import PartitionSpec as P

ANSWERS = 4


def attend_part(queries, keys, values, allowed, scale_factor):
    scores = (
        jnp.einsum("ctkgd,cjkd->ckgtj", queries, keys, preferred_element_type=jnp.float32)
        * scale_factor
    )
    scores = jnp.where(allowed[None, None, None, :, :], scores, -jnp.inf)
    row_max = jnp.max(scores, axis=-1)
    expo = jnp.exp(scores - row_max[..., None])
    total = jnp.sum(expo, axis=-1)
    weights = expo.astype(jnp.bfloat16)
    summed = jnp.einsum("ckgtj,cjkd->ctkgd", weights, values, preferred_element_type=jnp.float32)
    return (row_max, total, summed)


def to_rows(stat):
    return jnp.transpose(stat, (0, 3, 1, 2))[..., None]


def per_device(
    cont_queries,
    cont_keys,
    cont_values,
    prefix_kv,
    probe,
    question_row,
    cont_slot,
    cont_length,
    gold,
):
    cont_count, clen, heads_here, head_dim = cont_queries.shape
    kv_here = cont_keys.shape[2]
    group_size = heads_here // kv_here
    quest_here = prefix_kv.shape[0]
    pref_len = prefix_kv.shape[2]
    questions = question_row.shape[0]
    scale_factor = 1.0 / head_dim**0.5
    wanted = question_row[cont_slot // ANSWERS]
    piece = lax.all_gather(prefix_kv, "wide", axis=0, tiled=True)
    count = piece.shape[0]
    hits = (wanted[:, None] == jnp.arange(count, dtype=jnp.int32)[None, :]).astype(jnp.bfloat16)
    chosen = jnp.einsum("cn,nkpvd->ckpvd", hits, piece, preferred_element_type=jnp.float32)
    mine = chosen.astype(jnp.bfloat16)
    queries = cont_queries.reshape(cont_count, clen, kv_here, group_size, head_dim)
    causal = jnp.arange(clen)[:, None] >= jnp.arange(clen)[None, :]
    keys_all = jnp.concatenate([mine[:, 0], cont_keys], axis=1)
    values_all = jnp.concatenate([mine[:, 1], cont_values], axis=1)
    allowed = jnp.concatenate([jnp.ones((clen, pref_len), dtype=bool), causal], axis=1)
    row_max, total, summed = attend_part(queries, keys_all, values_all, allowed, scale_factor)
    output = summed / to_rows(total)
    attended = output.astype(jnp.bfloat16).reshape(cont_count, clen, heads_here, head_dim)
    partial_value = jnp.einsum("cthd,hd->ct", attended, probe, preferred_element_type=jnp.float32)
    token_score = lax.psum(partial_value, "narrow")
    valid = jnp.arange(clen)[None, :] < cont_length[:, None]
    choice_score = jnp.sum(jnp.where(valid, token_score, 0.0), axis=1)
    target = wanted * ANSWERS + cont_slot % ANSWERS
    spots = target[:, None] == jnp.arange(questions * ANSWERS, dtype=jnp.int32)[None, :]
    term = jnp.sum(jnp.where(spots, choice_score[:, None], 0.0), axis=0).reshape(questions, ANSWERS)
    first_row = lax.axis_index("wide") * quest_here
    totals = lax.psum(term, "wide")
    owned = lax.dynamic_slice_in_dim(totals, first_row, quest_here, 0)
    logprob = owned - jax.nn.logsumexp(owned, axis=1, keepdims=True)
    owned_rows = first_row + jnp.arange(quest_here, dtype=jnp.int32)
    matches = question_row[None, :] == owned_rows[:, None]
    gold_owned = jnp.sum(jnp.where(matches, gold[None, :], 0), axis=1)
    answer_ids = jnp.arange(ANSWERS, dtype=jnp.int32)[None, :]
    owned_loss = -jnp.sum(jnp.where(answer_ids == gold_owned[:, None], logprob, 0.0), axis=1)
    return (token_score, logprob, owned_loss)


def solution(mesh):
    return jax.shard_map(
        per_device,
        mesh=mesh,
        in_specs=(
            P(("groups", "wide"), None, "narrow", None),
            P(("groups", "wide"), None, "narrow", None),
            P(("groups", "wide"), None, "narrow", None),
            P(("groups", "wide"), None, None, "narrow", None),
            P("narrow", None),
            P("groups"),
            P(("groups", "wide")),
            P(("groups", "wide")),
            P("groups"),
        ),
        out_specs=(P(("groups", "wide"), None), P(("groups", "wide"), None), P(("groups", "wide"))),
        check_vma=False,
    )
```

profile of v0, /device:TPU:0, one launch (start us, length us, event | category | flops | bytes accessed | tf_op | source)
XLA Modules:
  0.0 57.5 jit_solution(3568872146050696365)
XLA Ops:
  0.6 0.0 copy-start
  0.6 0.8 %compare_select_fusion = s32[4]{0:T(128)S(1)} fusion(s32[4]{0:T(128)} %param.15), kind=kLoop, calls=%fused_computation.27 | loop fusion | flops 72 | bytes 32 | tf_op jit(solution)/shard_map/select_n | solution.py:45
  1.5 1.3 %gather_fusion = s32[4]{0:T(128)S(1)} fusion(s32[4]{0:T(128)} %param.14, s32[1024]{0:T(1024)S(1)} %pad_clamp_fusion), kind=kCustom, calls=%fused_computation | custom fusion | bytes 48 | tf_op jit(solution)/shard_map/gather | solution.py:45
  2.8 0.9 %copy.34 = bf16[1,2,128,2,128]{4,2,3,1,0:T(8,128)(2,1)S(1)} copy(bf16[1,2,128,2,128]{4,3,2,1,0:T(2,128)(2,1)} %param.12) | data formatting | bytes 262144 | tf_op args[3]
  3.7 17.4 %all_gather.3 = bf16[4,2,128,2,128]{4,2,3,1,0:T(8,128)(2,1)S(1)} all-gather(bf16[1,2,128,2,128]{4,2,3,1,0:T(8,128)(2,1)S(1)} %copy.34), channel_id=1, replica_groups=mesh['groups'=2,'wide'=4,'narrow'=4] {'wide'}, dimensions={0}, use_global_device_ids=true | all-gather | bytes 655360 | tf_op jit(solution)/shard_map/all_gather | solution.py:46
  21.1 0.5 convolution_convert_fusion
  21.6 0.2 slice_bitcast_fusion.1
  21.8 1.3 %copy.36 = bf16[4,128,2,128]{3,0,2,1:T(4,128)(2,1)S(1)} copy(bf16[4,128,2,128]{3,2,1,0:T(2,128)(2,1)} %param.11) | data formatting | bytes 524288 | tf_op args[2]
  23.1 1.3 %copy.37 = bf16[4,128,2,128]{3,0,2,1:T(4,128)(2,1)S(1)} copy(bf16[4,128,2,128]{3,2,1,0:T(2,128)(2,1)} %param.10) | data formatting | bytes 524288 | tf_op args[1]
  24.4 0.7 %maximum_bitcast_fusion = (bf16[4,256,2,128,1]{3,0,2,1,4:T(4,128)(2,1)S(1)}, bf16[4,256,2,128,1]{3,0,2,1,4:T(4,128)(2,1)S(1)}) fusion(bf16[4,128,2,128]{3,0,2,1:T(4,128)(2,1)S(1)} %copy.36, bf16[4,128,2,128]{3,0,2,1:T(4,128)(2,1)S(1)} %get-tuple-element.5, bf16[4,128,2,128]{3,0,2,1:T(4,128)(2,1)S(1)} %copy.37, bf16[4,128,2,128]{3,0,2,1:T(4,128)(2,1)S(1)} %get-tuple-element.6), kind=kLoop, calls=%fused_computation.16 | loop fusion | flops 524288 | bytes 2097152 | tf_op jit(solution)/shard_map/concatenate | solution.py:54
  25.1 0.0 copy-done
  25.1 1.5 %fusion.2 = (f32[4,2,8,128]{3,2,1,0:T(8,128)S(1)}, f32[4,2,256,128,8]{3,2,4,1,0:T(8,128)S(1)}) fusion(pred[128,256]{0,1:T(8,128)(4,1)S(1)} %concatenate.10, bf16[4,128,2,8,128]{4,3,2,1,0:T(8,128)(2,1)S(1)} %bitcast.41, bf16[4,256,2,128,1]{3,0,2,1,4:T(4,128)(2,1)S(1)} %get-tuple-element.10), kind=kOutput, calls=%fused_computation.5 | convolution fusion | flops 543154176 | bytes 11075584 | tf_op jit(solution)/shard_map/ctkgd,cjkd->ckgtj/dot_general | solution.py:11
  26.7 2.2 %fusion = f32[4,2,8,128]{3,2,1,0:T(8,128)S(1)} fusion(f32[4,2,256,128,8]{3,2,4,1,0:T(8,128)S(1)} %get-tuple-element.8, f32[4,2,8,128]{3,2,1,0:T(8,128)S(1)} %get-tuple-element.7, pred[128,256]{0,1:T(8,128)(4,1)S(1)} %concatenate.10), kind=kLoop, calls=%fused_computation.3 | loop fusion | flops 8380416 | bytes 8486912 | tf_op jit(solution)/shard_map/reduce_sum | solution.py:17
  28.9 0.0 copy-start.2
  28.9 0.0 copy-start.4
  28.9 0.0 copy-start.6
  29.0 0.0 copy-start.1
  29.0 0.0 copy-start.5
  29.0 2.4 %fusion.5 = bf16[4,128,2,8,128]{1,4,3,2,0:T(8,128)(2,1)S(1)} fusion(f32[4,128,2,8]{1,3,2,0:T(8,128)S(1)} %bitcast.43, f32[4,2,256,128,8]{3,2,4,1,0:T(8,128)S(1)} %get-tuple-element.8, f32[4,2,8,128]{3,2,1,0:T(8,128)S(1)} %get-tuple-element.7, pred[128,256]{0,1:T(8,128)(4,1)S(1)} %concatenate.10, bf16[4,256,2,128,1]{3,0,2,1,4:T(4,128)(2,1)S(1)} %get-tuple-element.9), kind=kOutput, calls=%fused_computation.8 | convolution fusion | flops 547356672 | bytes 11108352 | tf_op jit(solution)/shard_map/ckgtj,cjkd->ctkgd/dot_general | solution.py:19
  31.3 0.0 copy-done.2
  31.3 0.4 fusion.17
  31.7 5.6 %psum.14 = f32[4,128]{1,0:T(4,128)S(1)} all-reduce(f32[4,128]{1,0:T(4,128)S(1)} %bitcast.45), channel_id=1, replica_groups=mesh['groups'=2,'wide'=4,'narrow'=4] {'narrow'}, use_global_device_ids=true, to_apply=%region_2.3 | all-reduce | flops 512 | bytes 4096 | tf_op jit(solution)/shard_map/psum | solution.py:60
  37.4 0.0 copy-done.4
  37.4 0.0 copy-start.3
  37.4 0.2 select_reduce_fusion.1
  37.6 0.0 copy-done.6
  37.6 0.1 select_reduce_fusion
  37.7 0.1 reshape.54
  37.7 12.5 %psum.15 = f32[4,4]{1,0:T(4,128)S(1)} all-reduce(f32[4,4]{1,0:T(4,128)S(1)} %reshape.54), channel_id=1, replica_groups=mesh['groups'=2,'wide'=4,'narrow'=4] {'wide'}, use_global_device_ids=true, to_apply=%region_5.6 | all-reduce | flops 16 | bytes 128 | tf_op jit(solution)/shard_map/psum | solution.py:67
  50.2 0.6 %fusion.27 = f32[]{:T(128)} fusion(f32[4,4]{1,0:T(4,128)S(1)} %psum.15, s32[]{:T(128)S(6)} %select_n.48), kind=kLoop, calls=%fused_computation.50 | loop fusion | flops 3 | bytes 24 | tf_op jit(solution)/shard_map/reduce_max | solution.py:69
  52.1 0.6 %exponential_reduce_fusion = f32[]{:T(128)} fusion(f32[]{:T(128)} %bitcast.15, f32[4,4]{1,0:T(4,128)S(1)} %psum.15, s32[]{:T(128)S(6)} %select_n.48), kind=kLoop, calls=%fused_computation.45 | loop fusion | flops 7 | bytes 28 | tf_op jit(solution)/shard_map/reduce_sum | solution.py:69
  53.4 0.0 copy-done.1
  53.4 0.0 copy-done.5
  53.4 0.6 %fusion.23 = s32[]{:T(128)} fusion(s32[4]{0:T(128)S(1)} %copy-done.5, s32[4]{0:T(128)S(1)} %copy-done.1, s32[]{:T(128)S(6)} %axis_index.15), kind=kLoop, calls=%fused_computation.43 | loop fusion | flops 11 | bytes 40 | tf_op jit(solution)/shard_map/reduce_sum | solution.py:72
  54.1 1.8 %fusion.24 = (f32[]{:T(128)}, f32[1,4]{1,0:T(1,128)}) fusion(s32[]{:T(128)} %fusion.23, f32[]{:T(128)} %bitcast.17, f32[4,4]{1,0:T(4,128)S(1)} %psum.15, s32[]{:T(128)S(6)} %select_n.48), kind=kLoop, calls=%fused_computation.44 | loop fusion | flops 15 | bytes 48 | tf_op jit(solution)/shard_map/reduce_sum | solution.py:74
  56.4 0.0 copy-done.3
  (4 shorter events, 0.0 us)
Async XLA Ops:
  0.6 24.5 %copy-start = (bf16[4,128,16,128]{3,2,1,0:T(8,128)(2,1)S(1)}, bf16[4,128,16,128]{3,2,1,0:T(8,128)(2,1)}, u32[]{:S(2)}) copy-start(bf16[4,128,16,128]{3,2,1,0:T(8,128)(2,1)} %param.9) | copy-start | bytes 6291460
  28.9 2.4 %copy-start.2 = (bf16[16,128]{1,0:T(8,128)(2,1)S(1)}, bf16[16,128]{1,0:T(8,128)(2,1)}, u32[]{:S(2)}) copy-start(bf16[16,128]{1,0:T(8,128)(2,1)} %param.13) | copy-start | bytes 12292
  28.9 8.4 %copy-start.4 = (s32[4]{0:T(128)S(1)}, s32[4]{0:T(128)}, u32[]{:S(2)}) copy-start(s32[4]{0:T(128)} %param.16) | copy-start | bytes 52
  28.9 8.6 %copy-start.6 = (s32[4]{0:T(128)S(1)}, s32[4]{0:T(128)}, u32[]{:S(2)}) copy-start(s32[4]{0:T(128)} %param.15) | copy-start | bytes 52
  29.0 24.5 %copy-start.1 = (s32[4]{0:T(128)S(1)}, s32[4]{0:T(128)}, u32[]{:S(2)}) copy-start(s32[4]{0:T(128)} %param.14) | copy-start | bytes 52
  29.0 24.5 %copy-start.5 = (s32[4]{0:T(128)S(1)}, s32[4]{0:T(128)}, u32[]{:S(2)}) copy-start(s32[4]{0:T(128)} %param.17) | copy-start | bytes 52
  37.4 19.0 %copy-start.3 = (f32[4,128]{1,0:T(4,128)}, f32[4,128]{1,0:T(4,128)S(1)}, u32[]{:S(2)}) copy-start(f32[4,128]{1,0:T(4,128)S(1)} %psum.14) | copy-start | bytes 6148
where the time goes:
time: 57.8 us; the launch traced here: 57.5 us
  blocking collectives  35.5 us (61%)
  other arithmetic  7.63 us (13%)
  local copies, waits for them, and re-layouts  5.13 us (9%)
  matrix products  4.82 us (8%)
  between operations  4.47 us (8%)
    all_gather x1, blocking collectives, per_device(): piece = lax.all_gather(prefix_kv, 'wide', axis=0, tiled=True)  17.4 us
    psum x1, blocking collectives, per_device(): totals = lax.psum(term, 'wide')  12.5 us
    psum x1, blocking collectives, per_device(): token_score = lax.psum(partial_value, 'narrow')  5.64 us
    unnamed x17, local copies, waits for them, and re-layouts  3.56 us
    dot_general x1, matrix products, attend_part(): jnp.einsum('ckgtj,cjkd->ctkgd', weights, values, preferred_element_type=j...  2.35 us
    reduce_sum x1, other arithmetic, attend_part(): total = jnp.sum(expo, axis=-1)  2.23 us
    reduce_sum x1, other arithmetic, per_device(): jnp.sum(jnp.where(answer_ids == gold_owned[:, None], logprob, 0.0), axis=1)  1.75 us
    dot_general x1, matrix products, attend_part(): jnp.einsum('ctkgd,cjkd->ckgtj', queries, keys, preferred_element_type=jnp...  1.54 us

commit v1 on v0

v1 whole, which is shorter than its diff:
```python
import math

import jax
import jax.numpy as jnp
from jax import lax
from jax.experimental import pallas as pl
from jax.experimental.pallas import tpu as pltpu
from jax.sharding import PartitionSpec as P

ANSWERS = 4
DIRECT_LIMIT = 8
F32 = jnp.float32
BF16 = jnp.bfloat16


def dot_nt(a, b):
    return lax.dot_general(a, b, (((1,), (1,)), ((), ())), preferred_element_type=F32)


def dot_tn(a, b):
    return lax.dot_general(a, b, (((0,), (0,)), ((), ())), preferred_element_type=F32)


def column_chunk(clen, group_size):
    cols = clen * group_size
    return 256 if cols % 256 == 0 else cols


def pack_kernel(prefix_ref, probe_ref, out_ref):
    pref_len, kv_here, head_dim = prefix_ref.shape[2:]
    heads_here = probe_ref.shape[0]
    group = heads_here // kv_here
    reads = []
    for k in range(kv_here):
        out_ref[0, k * pref_len : (k + 1) * pref_len, :] = prefix_ref[0, 0, :, k, :]
        reads.append(dot_nt(probe_ref[k * group : (k + 1) * group, :], prefix_ref[0, 1, :, k, :]))
    read = jnp.concatenate(reads, axis=0)
    high = read.astype(BF16)
    low = (read - high.astype(F32)).astype(BF16)
    base = kv_here * pref_len
    out_ref[0, base : base + heads_here, :] = high
    out_ref[0, base + heads_here : base + 2 * heads_here, :] = low


def own_kernel(query_ref, key_ref, value_ref, probe_ref, stat_ref):
    clen, kv_here, head_dim = key_ref.shape[1:]
    group = query_ref.shape[2] // kv_here
    cols = clen * group
    chunk = column_chunk(clen, group)
    span = chunk // group
    factor = math.log2(math.e) / math.sqrt(head_dim)
    row = lax.broadcasted_iota(jnp.int32, (span, chunk), 0)
    col = lax.broadcasted_iota(jnp.int32, (span, chunk), 1)
    seen = row * group <= col
    for k in range(kv_here):
        keys = key_ref[0, :, k, :]
        probe = probe_ref[k * group : (k + 1) * group, :]
        read = dot_nt(value_ref[0, :, k, :], jnp.concatenate([probe] * (chunk // group), axis=0))
        for start in range(0, cols, chunk):
            first = start // group
            last = first + span
            query = query_ref[0, first:last, k * group : (k + 1) * group, :].reshape(chunk, head_dim)
            scores = dot_nt(keys[:last], query)
            edge = jnp.where(seen, scores[first:last], -jnp.inf)
            scores = edge if first == 0 else jnp.concatenate([scores[:first], edge], axis=0)
            top = jnp.max(scores, axis=0, keepdims=True)
            expo = jnp.exp2((scores - top) * factor)
            total = jnp.sum(expo, axis=0, keepdims=True)
            summed = jnp.sum(expo * read[:last], axis=0, keepdims=True)
            stat_ref[0, 3 * k : 3 * k + 1, start : start + chunk] = top
            stat_ref[0, 3 * k + 1 : 3 * k + 2, start : start + chunk] = total
            stat_ref[0, 3 * k + 2 : 3 * k + 3, start : start + chunk] = summed


def prefix_kernel(source_ref, place_ref, target_ref, length_ref, query_ref, stat_ref, *rest, sources):
    piece_refs = rest[:sources]
    out_ref, cache, outcome, sem = rest[sources:]
    cont_count = cache.shape[0]
    c = pl.program_id(0)
    clen, heads_here, head_dim = query_ref.shape[1:]
    kv_here = stat_ref.shape[1] // 3
    group = heads_here // kv_here
    cols = clen * group
    chunk = column_chunk(clen, group)
    span = chunk // group
    pref_len = (cache.shape[1] - 2 * heads_here) // kv_here
    factor = math.log2(math.e) / math.sqrt(head_dim)

    @pl.when(c == 0)
    def _():
        outcome[...] = jnp.zeros(outcome.shape, F32)
        for i in range(cont_count):
            for s in range(sources):

                @pl.when(source_ref[i] == s)
                def _():
                    pltpu.make_async_copy(piece_refs[s].at[place_ref[i]], cache.at[i], sem.at[i]).start()

        for i in range(cont_count):
            pltpu.make_async_copy(piece_refs[0].at[0], cache.at[i], sem.at[i]).wait()

    base = kv_here * pref_len
    pick_row = lax.broadcasted_iota(jnp.int32, (heads_here, chunk), 0)
    pick_col = lax.broadcasted_iota(jnp.int32, (heads_here, chunk), 1)
    parts = [None] * (cols // chunk)
    for k in range(kv_here):
        keys = cache[c, k * pref_len : (k + 1) * pref_len, :]
        pick = (pick_row == pick_col % group + k * group).astype(F32).astype(BF16)
        read = dot_tn(cache[c, base : base + heads_here, :], pick) + dot_tn(
            cache[c, base + heads_here : base + 2 * heads_here, :], pick
        )
        for n in range(cols // chunk):
            start = n * chunk
            first = start // group
            query = query_ref[0, first : first + span, k * group : (k + 1) * group, :].reshape(chunk, head_dim)
            scores = dot_nt(keys, query)
            own_top = stat_ref[0, 3 * k : 3 * k + 1, start : start + chunk]
            own_total = stat_ref[0, 3 * k + 1 : 3 * k + 2, start : start + chunk]
            own_sum = stat_ref[0, 3 * k + 2 : 3 * k + 3, start : start + chunk]
            top = jnp.maximum(jnp.max(scores, axis=0, keepdims=True), own_top)
            expo = jnp.exp2((scores - top) * factor)
            shrink = jnp.exp2((own_top - top) * factor)
            total = jnp.sum(expo, axis=0, keepdims=True) + own_total * shrink
            summed = jnp.sum(expo * read, axis=0, keepdims=True) + own_sum * shrink
            value = summed / total
            parts[n] = value if parts[n] is None else parts[n] + value
    for n in range(cols // chunk):
        outcome[pl.ds(c, 1), n * chunk : (n + 1) * chunk] = parts[n]

    @pl.when(c == cont_count - 1)
    def _():
        values = outcome[...]
        where_row = lax.broadcasted_iota(jnp.int32, (cols, clen), 0)
        where_col = lax.broadcasted_iota(jnp.int32, (cols, clen), 1)
        fold = (where_row // group == where_col).astype(F32).astype(BF16)
        high = values.astype(BF16).astype(F32)
        middle = (values - high).astype(BF16).astype(F32)
        low = values - high - middle
        stacked = jnp.concatenate([high, middle, low], axis=0).astype(BF16)
        folded = lax.dot_general(stacked, fold, (((1,), (0,)), ((), ())), preferred_element_type=F32)
        rows = outcome.shape[0]
        token = folded[:rows] + folded[rows : 2 * rows] + folded[2 * rows :]
        out_ref[0 : token.shape[0], :] = token
        lane = lax.broadcasted_iota(jnp.int32, (1, clen), 1)
        spot_rows = out_ref.shape[0] - rows
        spot = lax.broadcasted_iota(jnp.int32, (spot_rows, clen), 0) * clen + lax.broadcasted_iota(
            jnp.int32, (spot_rows, clen), 1
        )
        term = jnp.zeros((spot_rows, clen), F32)
        for i in range(cont_count):
            kept = jnp.where(lane < length_ref[i], token[i : i + 1], 0.0)
            choice = jnp.sum(kept, axis=1, keepdims=True)
            term = term + jnp.where(spot == target_ref[i], choice, 0.0)
        out_ref[rows:, :] = term


def shift(x, axis, by, size):
    return lax.ppermute(x, axis, [(i, (i + by) % size) for i in range(size)])


def swap(x, axis, bit, size):
    return lax.ppermute(x, axis, [(i, i ^ bit) for i in range(size)])


def exchange_sum(x, axis, size):
    if size > DIRECT_LIMIT:
        return lax.psum(x, axis)
    return x + sum(shift(x, axis, by, size) for by in range(1, size))


def doubling_sum(x, axis, size):
    if size & (size - 1):
        return lax.psum(x, axis)
    bit = 1
    while bit < size:
        x = x + swap(x, axis, bit, size)
        bit *= 2
    return x


def per_device(mesh_shape, *args):
    (cont_queries, cont_keys, cont_values, prefix_kv, probe, question_row, cont_slot, cont_length, gold) = args
    wide, narrow = mesh_shape["wide"], mesh_shape["narrow"]
    cont_count, clen, heads_here, head_dim = cont_queries.shape
    kv_here = cont_keys.shape[2]
    group = heads_here // kv_here
    cols = clen * group
    quest_here, _, pref_len = prefix_kv.shape[:3]
    questions = question_row.shape[0]
    packed_rows = kv_here * pref_len + 2 * heads_here

    packed = pl.pallas_call(
        pack_kernel,
        grid=(quest_here,),
        in_specs=[
            pl.BlockSpec((1, 2, pref_len, kv_here, head_dim), lambda i: (i, 0, 0, 0, 0)),
            pl.BlockSpec((heads_here, head_dim), lambda i: (0, 0)),
        ],
        out_specs=pl.BlockSpec((1, packed_rows, head_dim), lambda i: (i, 0, 0)),
        out_shape=jax.ShapeDtypeStruct((quest_here, packed_rows, head_dim), BF16),
        name="pack",
    )(prefix_kv, probe)

    wanted = question_row[cont_slot // ANSWERS].astype(jnp.int32)
    me = lax.axis_index("wide")
    if wide <= DIRECT_LIMIT:
        pieces = [packed] + [shift(packed, "wide", by, wide) for by in range(1, wide)]
        source = (me - wanted // quest_here) % wide
        place = wanted % quest_here
    else:
        pieces = [lax.all_gather(packed, "wide", axis=0, tiled=True)]
        source = jnp.zeros_like(wanted)
        place = wanted

    stat_rows = 3 * kv_here
    stats = pl.pallas_call(
        own_kernel,
        grid=(cont_count,),
        in_specs=[
            pl.BlockSpec((1, clen, heads_here, head_dim), lambda i: (i, 0, 0, 0)),
            pl.BlockSpec((1, clen, kv_here, head_dim), lambda i: (i, 0, 0, 0)),
            pl.BlockSpec((1, clen, kv_here, head_dim), lambda i: (i, 0, 0, 0)),
            pl.BlockSpec((heads_here, head_dim), lambda i: (0, 0)),
        ],
        out_specs=pl.BlockSpec((1, stat_rows, cols), lambda i: (i, 0, 0)),
        out_shape=jax.ShapeDtypeStruct((cont_count, stat_rows, cols), F32),
        cost_estimate=pl.CostEstimate(flops=10**9, bytes_accessed=3 * 10**6, transcendentals=10**6),
        name="own",
    )(cont_queries, cont_keys, cont_values, probe)

    target = wanted * ANSWERS + cont_slot % ANSWERS
    spot_rows = -(-questions * ANSWERS // clen)
    rows = -(-cont_count // 8) * 8
    payload = pl.pallas_call(
        lambda *refs: prefix_kernel(*refs, sources=len(pieces)),
        grid_spec=pltpu.PrefetchScalarGridSpec(
            num_scalar_prefetch=4,
            grid=(cont_count,),
            in_specs=[
                pl.BlockSpec((1, clen, heads_here, head_dim), lambda i, *_: (i, 0, 0, 0)),
                pl.BlockSpec((1, stat_rows, cols), lambda i, *_: (i, 0, 0)),
            ]
            + [pl.BlockSpec(memory_space=pl.ANY)] * len(pieces),
            out_specs=pl.BlockSpec((rows + 8 * (-(-spot_rows // 8)), clen), lambda i, *_: (0, 0)),
            scratch_shapes=[
                pltpu.VMEM((cont_count, packed_rows, head_dim), BF16),
                pltpu.VMEM((rows, cols), F32),
                pltpu.SemaphoreType.DMA((cont_count,)),
            ],
        ),
        out_shape=jax.ShapeDtypeStruct((rows + 8 * (-(-spot_rows // 8)), clen), F32),
        name="prefix",
    )(source, place, target, cont_length, cont_queries, stats, *pieces)

    summed = exchange_sum(payload, "narrow", narrow)
    token_score = summed[:cont_count]
    totals = doubling_sum(summed[rows : rows + spot_rows], "wide", wide)
    totals = totals.reshape(-1)[: questions * ANSWERS].reshape(questions, ANSWERS)
    first_row = me * quest_here
    owned = lax.dynamic_slice_in_dim(totals, first_row, quest_here, 0)
    logprob = owned - jax.nn.logsumexp(owned, axis=1, keepdims=True)
    owned_rows = first_row + jnp.arange(quest_here, dtype=jnp.int32)
    matches = question_row[None, :] == owned_rows[:, None]
    gold_owned = jnp.sum(jnp.where(matches, gold[None, :], 0), axis=1)
    answer_ids = jnp.arange(ANSWERS, dtype=jnp.int32)[None, :]
    owned_loss = -jnp.sum(jnp.where(answer_ids == gold_owned[:, None], logprob, 0.0), axis=1)
    return (token_score, logprob, owned_loss)


def solution(mesh):
    shape = dict(mesh.shape)
    return jax.shard_map(
        lambda *args: per_device(shape, *args),
        mesh=mesh,
        in_specs=(
            P(("groups", "wide"), None, "narrow", None),
            P(("groups", "wide"), None, "narrow", None),
            P(("groups", "wide"), None, "narrow", None),
            P(("groups", "wide"), None, None, "narrow", None),
            P("narrow", None),
            P("groups"),
            P(("groups", "wide")),
            P(("groups", "wide")),
            P("groups"),
        ),
        out_specs=(P(("groups", "wide"), None), P(("groups", "wide"), None), P(("groups", "wide"))),
        check_vma=False,
    )
```

time: 57.8 us -> 45.2 us (0.78)
  blocking collectives: 35.5 us -> 0 us
  Pallas kernels: 0 us -> 13.2 us
  starting transfers between devices: 0 us -> 11 us
  waiting for transfers between devices: 0 us -> 7.4 us
  matrix products: 4.82 us -> 0 us
  local copies, waits for them, and re-layouts: 5.13 us -> 2.64 us
  other arithmetic: 7.63 us -> 6.2 us
    psum x2 -> x0, blocking collectives: 18.1 us -> none  [the longest x1 12.5 us: per_device(): totals = lax.psum(term, 'wide')]
    all_gather x1 -> x0, blocking collectives: 17.4 us -> none  [per_device(): piece = lax.all_gather(prefix_kv, 'wide', axis=0, tiled=True)]
    pallas_call x0 -> x3, Pallas kernels: none -> 13.2 us  [the longest x1 6.32 us: per_device(): pl.pallas_call(lambda *refs: prefix_kernel(*refs, sources=len(pieces)), g...]
    ppermute x0 -> x8, starting transfers between devices: none -> 11 us  [the longest x6 10 us: shift(): return lax.ppermute(x, axis, [(i, (i + by) % size) for i in range(size)])]
    ppermute x0 -> x8, waiting for transfers between devices: none -> 7.4 us  [the longest x2 5.82 us: swap(): return lax.ppermute(x, axis, [(i, i ^ bit) for i in range(size)])]
    dot_general x4 -> x0, matrix products: 4.82 us -> none  [the longest x1 2.35 us: attend_part(): jnp.einsum('ckgtj,cjkd->ctkgd', weights, values, preferred_element_type=j...]
    unnamed x17 -> x10, local copies, waits for them, and re-layouts: 3.56 us -> 0.12 us
    reduce_sum x3 -> x0, other arithmetic: 2.49 us -> none  [the longest x1 2.23 us: attend_part(): total = jnp.sum(expo, axis=-1)]
  transfers between devices with their start and end apart: 0 -> 8, of which waited for: 0 -> 5; matrix products, arithmetic and copies ran while one was open for 0% -> 10% of each run, Pallas kernels for 0% -> 10%
where the time goes in v1:
time: 45.2 us; the launch traced here: 44.8 us
  Pallas kernels  13.2 us (29%)
  starting transfers between devices  11 us (24%)
  waiting for transfers between devices  7.4 us (16%)
  other arithmetic  6.2 us (14%)
  between operations  4.38 us (10%)
  local copies, waits for them, and re-layouts  2.64 us (6%)
    ppermute x6, starting transfers between devices, shift(): return lax.ppermute(x, axis, [(i, (i + by) % size) for i in range(size)])  10 us
    pallas_call x1, Pallas kernels, per_device(): pl.pallas_call(lambda *refs: prefix_kernel(*refs, sources=len(pieces)), g...  6.32 us
    ppermute x2, waiting for transfers between devices, swap(): return lax.ppermute(x, axis, [(i, i ^ bit) for i in range(size)])  5.82 us
    pallas_call x1, Pallas kernels, per_device(): pl.pallas_call(own_kernel, grid=(cont_count,), in_specs=[pl.BlockSpec((1,...  4.67 us
    pallas_call x1, Pallas kernels, per_device(): pl.pallas_call(pack_kernel, grid=(quest_here,), in_specs=[pl.BlockSpec((1...  2.18 us
    reduce_sum x1, other arithmetic, per_device(): jnp.sum(jnp.where(answer_ids == gold_owned[:, None], logprob, 0.0), axis=1)  1.79 us
    ppermute x6, waiting for transfers between devices, shift(): return lax.ppermute(x, axis, [(i, (i + by) % size) for i in range(size)])  1.58 us
    gather x1, local copies, waits for them, and re-layouts, per_device(): wanted = question_row[cont_slot // ANSWERS].astype(jnp.int32)  1.29 us
  transfers between devices with their start and end apart: 8, of which 5 were waited for; matrix products, arithmetic and copies ran while one was open for 10% of the time, Pallas kernels for 10%

profile of v1, /device:TPU:0, one launch (start us, length us, event | category | flops | bytes accessed | tf_op | source)
XLA Modules:
  0.0 44.8 jit_solution(16471250418274060233)
XLA Ops:
  0.6 2.2 %pack.1.refs_6_ = bf16[1,288,128]{2,1,0:T(8,128)(2,1)} custom-call(bf16[1,2,128,2,128]{4,3,2,1,0:T(2,128)(2,1)} %prefix_ref.1, bf16[16,128]{1,0:T(8,128)(2,1)} %probe_ref.3), custom_call_target="tpu_custom_call" | custom-call | tf_op jit(solution)/shard_map/pack/pallas_call | solution.py:192
  2.8 3.1 %collective-permute-start = (bf16[1,288,128]{2,1,0:T(8,128)(2,1)}, bf16[1,288,128]{2,1,0:T(8,128)(2,1)S(1)}, u32[]{:S(2)}, u32[]{:S(2)}) collective-permute-start(bf16[1,288,128]{2,1,0:T(8,128)(2,1)} %pack.1.refs_6_), channel_id=1, source_target_pairs={{0,4},{4,8},{8,12},{12,0},{1,5},{5,9},{9,13},{13,1},{2,6},{6,10},{... | collective-permute-start | bytes 221192 | tf_op jit(solution)/shard_map/ppermute | solution.py:158
  5.9 2.6 %collective-permute-start.1 = (bf16[1,288,128]{2,1,0:T(8,128)(2,1)}, bf16[1,288,128]{2,1,0:T(8,128)(2,1)S(1)}, u32[]{:S(2)}, u32[]{:S(2)}) collective-permute-start(bf16[1,288,128]{2,1,0:T(8,128)(2,1)} %pack.1.refs_6_), channel_id=1, source_target_pairs={{0,8},{4,12},{8,0},{12,4},{1,9},{5,13},{9,1},{13,5},{2,10},{6,14},... | collective-permute-start | bytes 221192 | tf_op jit(solution)/shard_map/ppermute | solution.py:158
  8.5 1.3 %collective-permute-start.2 = (bf16[1,288,128]{2,1,0:T(8,128)(2,1)}, bf16[1,288,128]{2,1,0:T(8,128)(2,1)S(1)}, u32[]{:S(2)}, u32[]{:S(2)}) collective-permute-start(bf16[1,288,128]{2,1,0:T(8,128)(2,1)} %pack.1.refs_6_), channel_id=1, source_target_pairs={{0,12},{4,0},{8,4},{12,8},{1,13},{5,1},{9,5},{13,9},{2,14},{6,2},{... | collective-permute-start | bytes 221192 | tf_op jit(solution)/shard_map/ppermute | solution.py:158
  9.8 0.7 %compare_select_fusion = s32[4]{0:T(128)S(1)} fusion(s32[4]{0:T(128)} %param.15), kind=kLoop, calls=%fused_computation.3 | loop fusion | flops 72 | bytes 32 | tf_op jit(solution)/shard_map/select_n | solution.py:204
  10.5 1.3 %gather_fusion = s32[4]{0:T(128)S(1)} fusion(s32[4]{0:T(128)} %param.14, s32[1024]{0:T(1024)S(1)} %pad_clamp_fusion), kind=kCustom, calls=%fused_computation | custom fusion | bytes 48 | tf_op jit(solution)/shard_map/gather | solution.py:204
  11.8 1.2 %fusion = (s32[4]{0:T(128)}, s32[4]{0:T(128)}) fusion(s32[4]{0:T(128)S(1)} %gather_fusion, s32[4]{0:T(128)} %param.15, s32[]{:T(128)S(6)} %axis_index.15), kind=kLoop, calls=%fused_computation.14 | loop fusion | flops 100 | bytes 68 | tf_op jit(solution)/shard_map/add | solution.py:231
  13.0 4.7 %own.1.refs_5_ = f32[4,6,1024]{2,1,0:T(8,128)} custom-call(bf16[4,128,16,128]{3,2,1,0:T(8,128)(2,1)} %refs_4_.1, bf16[4,128,2,128]{3,2,1,0:T(2,128)(2,1)} %key_ref.1, bf16[4,128,2,128]{3,2,1,0:T(2,128)(2,1)} %value_ref.1, bf16[16,128]{1,0:T(8,128)(2,1)} %probe_ref.3), custom_call_target="tpu_custom_call" | custom-call | flops 1000000000 | bytes 3000000 | tf_op jit(solution)/shard_map/own/pallas_call | solution.py:216
  17.6 0.0 copy-start
  17.6 0.0 copy-start.4
  17.6 0.0 collective-permute-done.refs_7_
  17.6 0.0 copy-start.1
  17.6 0.0 collective-permute-done.1.refs_8_
  17.7 0.0 copy-start.2
  17.7 0.0 collective-permute-done.2.refs_9_
  17.7 0.0 copy-start.3
  17.7 0.5 %rem.44.refs_1_ = s32[4]{0:T(128)} broadcast(s32[]{:T(128)} %constant.57.clone.1), dimensions={} | broadcast | bytes 20 | tf_op jit(solution)/shard_map/jit(floor_divide)/rem | solution.py:208
  18.2 0.0 copy-done.1
  18.3 0.0 copy-done.2
  18.3 0.0 copy-done.3
  18.3 6.3 %prefix.1 = f32[16,128]{1,0:T(8,128)} custom-call(s32[4]{0:T(128)} %get-tuple-element.6.refs_0_, s32[4]{0:T(128)} %rem.44.refs_1_, s32[4]{0:T(128)} %get-tuple-element.5.refs_2_, s32[4]{0:T(128)} %refs_3_.1, bf16[4,128,16,128]{3,2,1,0:T(8,128)(2,1)} %refs_4_.1, f32[4,6,1024]{2,1,0:T(8,128)} %own.1.refs_5_, bf16[1,288,128]{2,1,0:T(8,128)(2,1)} %pack.1.refs_6_, ...), custom_call_target="tpu_custom_call" | custom-call | tf_op jit(solution)/shard_map/prefix/pallas_call | solution.py:234
  24.7 0.1 collective-permute-start.3
  24.7 1.6 %collective-permute-start.4 = (f32[16,128]{1,0:T(8,128)}, f32[16,128]{1,0:T(8,128)S(1)}, u32[]{:S(2)}, u32[]{:S(2)}) collective-permute-start(f32[16,128]{1,0:T(8,128)} %prefix.1), channel_id=1, source_target_pairs={{0,2},{1,3},{2,0},{3,1},{4,6},{5,7},{6,4},{7,5},{8,10},{9,11},{10,... | collective-permute-start | bytes 24584 | tf_op jit(solution)/shard_map/ppermute | solution.py:158
  26.3 1.4 %collective-permute-start.5 = (f32[16,128]{1,0:T(8,128)}, f32[16,128]{1,0:T(8,128)S(1)}, u32[]{:S(2)}, u32[]{:S(2)}) collective-permute-start(f32[16,128]{1,0:T(8,128)} %prefix.1), channel_id=1, source_target_pairs={{0,3},{1,0},{2,1},{3,2},{4,7},{5,4},{6,5},{7,6},{8,11},{9,8},{10,9... | collective-permute-start | bytes 24584 | tf_op jit(solution)/shard_map/ppermute | solution.py:158
  27.7 0.3 collective-permute-done.3
  28.0 0.7 %collective-permute-done.4 = f32[16,128]{1,0:T(8,128)S(1)} collective-permute-done((f32[16,128]{1,0:T(8,128)}, f32[16,128]{1,0:T(8,128)S(1)}, u32[]{:S(2)}, u32[]{:S(2)}) %collective-permute-start.4) | collective-permute-done | bytes 8224 | tf_op jit(solution)/shard_map/ppermute | solution.py:158
  28.6 0.6 %collective-permute-done.5 = f32[16,128]{1,0:T(8,128)S(1)} collective-permute-done((f32[16,128]{1,0:T(8,128)}, f32[16,128]{1,0:T(8,128)S(1)}, u32[]{:S(2)}, u32[]{:S(2)}) %collective-permute-start.5) | collective-permute-done | bytes 8224 | tf_op jit(solution)/shard_map/ppermute | solution.py:158
  29.3 0.7 %add_add_fusion = f32[16,128]{1,0:T(8,128)S(1)} fusion(f32[16,128]{1,0:T(8,128)} %prefix.1, f32[16,128]{1,0:T(8,128)S(1)} %collective-permute-done.5, f32[16,128]{1,0:T(8,128)S(1)} %collective-permute-done.3, f32[16,128]{1,0:T(8,128)S(1)} %collective-permute-done.4), kind=kLoop, calls=%fused_computation.1 | loop fusion | flops 6144 | bytes 40960 | tf_op jit(solution)/shard_map/add | solution.py:168
  30.0 0.7 %collective-permute-start.6 = (f32[1,128]{1,0:T(1,128)S(1)}, f32[1,128]{1,0:T(1,128)S(1)}, u32[]{:S(2)}, u32[]{:S(2)}) collective-permute-start(f32[1,128]{1,0:T(1,128)S(1)} %slice.16), channel_id=1, source_target_pairs={{0,4},{4,0},{8,12},{12,8},{1,5},{5,1},{9,13},{13,9},{2,6},{6,2},{1... | collective-permute-start | bytes 1544 | tf_op jit(solution)/shard_map/ppermute | solution.py:162
  30.6 2.9 %collective-permute-done.6 = f32[1,128]{1,0:T(1,128)S(1)} collective-permute-done((f32[1,128]{1,0:T(1,128)S(1)}, f32[1,128]{1,0:T(1,128)S(1)}, u32[]{:S(2)}, u32[]{:S(2)}) %collective-permute-start.6) | collective-permute-done | bytes 544 | tf_op jit(solution)/shard_map/ppermute | solution.py:162
  33.5 0.3 collective-permute-start.7
  33.9 0.0 copy-done
  33.9 0.0 copy-done.4
  33.9 0.6 %fusion.1 = s32[]{:T(128)} fusion(s32[4]{0:T(128)S(1)} %copy-done.4, s32[4]{0:T(128)S(1)} %copy-done, s32[]{:T(128)S(6)} %axis_index.15), kind=kLoop, calls=%fused_computation.15 | loop fusion | flops 11 | bytes 40 | tf_op jit(solution)/shard_map/reduce_sum | solution.py:264
  34.5 0.6 %slice.15 = f32[4,128]{1,0:T(4,128)} slice(f32[16,128]{1,0:T(8,128)S(1)} %add_add_fusion), slice={[0:4], [0:128]} | slice | bytes 4096 | tf_op jit(solution)/shard_map/slice | solution.py:256
  35.1 2.9 %collective-permute-done.7 = f32[1,128]{1,0:T(1,128)S(1)} collective-permute-done((f32[1,128]{1,0:T(1,128)S(1)}, f32[1,128]{1,0:T(1,128)S(1)}, u32[]{:S(2)}, u32[]{:S(2)}) %collective-permute-start.7) | collective-permute-done | bytes 544 | tf_op jit(solution)/shard_map/ppermute | solution.py:162
  38.0 0.1 reshape.42
  38.1 0.6 %fusion.4 = f32[]{:T(128)} fusion(f32[4,4]{1,0:T(4,128)S(1)} %reshape.42, s32[]{:T(128)S(6)} %select_n.41), kind=kLoop, calls=%fused_computation.23 | loop fusion | flops 3 | bytes 24 | tf_op jit(solution)/shard_map/reduce_max | solution.py:261
  40.0 0.6 %exponential_reduce_fusion = f32[]{:T(128)} fusion(f32[]{:T(128)} %bitcast.1, f32[4,4]{1,0:T(4,128)S(1)} %reshape.42, s32[]{:T(128)S(6)} %select_n.41), kind=kLoop, calls=%fused_computation.18 | loop fusion | flops 7 | bytes 28 | tf_op jit(solution)/shard_map/reduce_sum | solution.py:261
  41.2 1.8 %fusion.2 = (f32[]{:T(128)}, f32[1,4]{1,0:T(1,128)}) fusion(s32[]{:T(128)} %fusion.1, f32[]{:T(128)} %bitcast.3, f32[4,4]{1,0:T(4,128)S(1)} %reshape.42, s32[]{:T(128)S(6)} %select_n.41), kind=kLoop, calls=%fused_computation.16 | loop fusion | flops 15 | bytes 48 | tf_op jit(solution)/shard_map/reduce_sum | solution.py:266
  (5 shorter events, 0.0 us)
Async XLA Ops:
  2.8 14.8 %collective-permute-start = (bf16[1,288,128]{2,1,0:T(8,128)(2,1)}, bf16[1,288,128]{2,1,0:T(8,128)(2,1)S(1)}, u32[]{:S(2)}, u32[]{:S(2)}) collective-permute-start(bf16[1,288,128]{2,1,0:T(8,128)(2,1)} %pack.1.refs_6_), channel_id=1, source_target_pairs={{0,4},{4,8},{8,12},{12,0},{1,5},{5,9},{9,13},{13,1},{2,6},{6,10},{... | collective-permute-start | bytes 221192 | tf_op jit(solution)/shard_map/ppermute | solution.py:158
  5.9 11.8 %collective-permute-start.1 = (bf16[1,288,128]{2,1,0:T(8,128)(2,1)}, bf16[1,288,128]{2,1,0:T(8,128)(2,1)S(1)}, u32[]{:S(2)}, u32[]{:S(2)}) collective-permute-start(bf16[1,288,128]{2,1,0:T(8,128)(2,1)} %pack.1.refs_6_), channel_id=1, source_target_pairs={{0,8},{4,12},{8,0},{12,4},{1,9},{5,13},{9,1},{13,5},{2,10},{6,14},... | collective-permute-start | bytes 221192 | tf_op jit(solution)/shard_map/ppermute | solution.py:158
  8.5 9.2 %collective-permute-start.2 = (bf16[1,288,128]{2,1,0:T(8,128)(2,1)}, bf16[1,288,128]{2,1,0:T(8,128)(2,1)S(1)}, u32[]{:S(2)}, u32[]{:S(2)}) collective-permute-start(bf16[1,288,128]{2,1,0:T(8,128)(2,1)} %pack.1.refs_6_), channel_id=1, source_target_pairs={{0,12},{4,0},{8,4},{12,8},{1,13},{5,1},{9,5},{13,9},{2,14},{6,2},{... | collective-permute-start | bytes 221192 | tf_op jit(solution)/shard_map/ppermute | solution.py:158
  17.6 16.2 %copy-start = (s32[4]{0:T(128)S(1)}, s32[4]{0:T(128)}, u32[]{:S(2)}) copy-start(s32[4]{0:T(128)} %param.14) | copy-start | bytes 52
  17.6 16.2 %copy-start.4 = (s32[4]{0:T(128)S(1)}, s32[4]{0:T(128)}, u32[]{:S(2)}) copy-start(s32[4]{0:T(128)} %param.17) | copy-start | bytes 52
  17.6 0.6 %copy-start.1 = (bf16[1,288,128]{2,1,0:T(8,128)(2,1)}, bf16[1,288,128]{2,1,0:T(8,128)(2,1)S(1)}, u32[]{:S(2)}) copy-start(bf16[1,288,128]{2,1,0:T(8,128)(2,1)S(1)} %collective-permute-done.refs_7_) | copy-start | bytes 221188
  17.7 0.6 %copy-start.2 = (bf16[1,288,128]{2,1,0:T(8,128)(2,1)}, bf16[1,288,128]{2,1,0:T(8,128)(2,1)S(1)}, u32[]{:S(2)}) copy-start(bf16[1,288,128]{2,1,0:T(8,128)(2,1)S(1)} %collective-permute-done.1.refs_8_) | copy-start | bytes 221188
  17.7 0.7 %copy-start.3 = (bf16[1,288,128]{2,1,0:T(8,128)(2,1)}, bf16[1,288,128]{2,1,0:T(8,128)(2,1)S(1)}, u32[]{:S(2)}) copy-start(bf16[1,288,128]{2,1,0:T(8,128)(2,1)S(1)} %collective-permute-done.2.refs_9_) | copy-start | bytes 221188
  24.7 3.3 %collective-permute-start.3 = (f32[16,128]{1,0:T(8,128)}, f32[16,128]{1,0:T(8,128)S(1)}, u32[]{:S(2)}, u32[]{:S(2)}) collective-permute-start(f32[16,128]{1,0:T(8,128)} %prefix.1), channel_id=1, source_target_pairs={{0,1},{1,2},{2,3},{3,0},{4,5},{5,6},{6,7},{7,4},{8,9},{9,10},{10,1... | collective-permute-start | bytes 24584 | tf_op jit(solution)/shard_map/ppermute | solution.py:158
  24.7 3.9 %collective-permute-start.4 = (f32[16,128]{1,0:T(8,128)}, f32[16,128]{1,0:T(8,128)S(1)}, u32[]{:S(2)}, u32[]{:S(2)}) collective-permute-start(f32[16,128]{1,0:T(8,128)} %prefix.1), channel_id=1, source_target_pairs={{0,2},{1,3},{2,0},{3,1},{4,6},{5,7},{6,4},{7,5},{8,10},{9,11},{10,... | collective-permute-start | bytes 24584 | tf_op jit(solution)/shard_map/ppermute | solution.py:158
  26.3 3.0 %collective-permute-start.5 = (f32[16,128]{1,0:T(8,128)}, f32[16,128]{1,0:T(8,128)S(1)}, u32[]{:S(2)}, u32[]{:S(2)}) collective-permute-start(f32[16,128]{1,0:T(8,128)} %prefix.1), channel_id=1, source_target_pairs={{0,3},{1,0},{2,1},{3,2},{4,7},{5,4},{6,5},{7,6},{8,11},{9,8},{10,9... | collective-permute-start | bytes 24584 | tf_op jit(solution)/shard_map/ppermute | solution.py:158
  30.0 3.6 %collective-permute-start.6 = (f32[1,128]{1,0:T(1,128)S(1)}, f32[1,128]{1,0:T(1,128)S(1)}, u32[]{:S(2)}, u32[]{:S(2)}) collective-permute-start(f32[1,128]{1,0:T(1,128)S(1)} %slice.16), channel_id=1, source_target_pairs={{0,4},{4,0},{8,12},{12,8},{1,5},{5,1},{9,13},{13,9},{2,6},{6,2},{1... | collective-permute-start | bytes 1544 | tf_op jit(solution)/shard_map/ppermute | solution.py:162
  33.5 4.5 %collective-permute-start.7 = (f32[1,128]{1,0:T(1,128)S(1)}, f32[1,128]{1,0:T(1,128)S(1)}, u32[]{:S(2)}, u32[]{:S(2)}) collective-permute-start(f32[1,128]{1,0:T(1,128)S(1)} %slice_add_fusion), channel_id=1, source_target_pairs={{0,8},{4,12},{8,0},{12,4},{1,9},{5,13},{9,1},{13,5},{2,10},{6,14},... | collective-permute-start | bytes 1544 | tf_op jit(solution)/shard_map/ppermute | solution.py:162

commit v2 on v0

v2 whole, which is shorter than its diff:
```python
import math

import jax
import jax.numpy as jnp
from jax import lax
from jax.experimental import pallas as pl
from jax.experimental.pallas import tpu as pltpu
from jax.sharding import PartitionSpec as P

ANSWERS = 4
DIRECT_LIMIT = 8
KERNEL_BYTES = 16 << 20
F32 = jnp.float32
BF16 = jnp.bfloat16


def dot_nt(a, b):
    return lax.dot_general(a, b, (((1,), (1,)), ((), ())), preferred_element_type=F32)


def dot_tn(a, b):
    return lax.dot_general(a, b, (((0,), (0,)), ((), ())), preferred_element_type=F32)


def split_heads(joined):
    rows, heads, depth = joined.shape
    flat = joined.reshape(rows * heads, depth)
    to = lax.broadcasted_iota(jnp.int32, (rows, rows * heads), 0)
    at = lax.broadcasted_iota(jnp.int32, (rows, rows * heads), 1)
    return [
        lax.dot_general(
            (at == to * heads + k).astype(F32).astype(BF16),
            flat,
            (((1,), (0,)), ((), ())),
            preferred_element_type=F32,
        ).astype(BF16)
        for k in range(heads)
    ]


def column_chunk(clen, group_size):
    cols = clen * group_size
    return 256 if cols % 256 == 0 else cols


def pack_kernel(prefix_ref, probe_ref, *refs):
    count = (len(refs) - 2) // 2
    moved, out_ref, kept, sem = refs[:count], refs[count], refs[count + 1 : -1], refs[-1]
    copies = [pltpu.make_async_copy(moved[i], kept[i], sem.at[i]) for i in range(count)]
    for copy in copies:
        copy.start()
    quest_here, _, pref_len, kv_here, head_dim = prefix_ref.shape
    heads_here = probe_ref.shape[0]
    group = heads_here // kv_here
    base = kv_here * pref_len

    def body(i, carry):
        reads = []
        keys, values = split_heads(prefix_ref[i, 0]), split_heads(prefix_ref[i, 1])
        for k in range(kv_here):
            out_ref[i, k * pref_len : (k + 1) * pref_len, :] = keys[k]
            reads.append(dot_nt(probe_ref[k * group : (k + 1) * group, :], values[k]))
        read = jnp.concatenate(reads, axis=0)
        high = read.astype(BF16)
        low = (read - high.astype(F32)).astype(BF16)
        out_ref[i, base : base + heads_here, :] = high
        out_ref[i, base + heads_here : base + 2 * heads_here, :] = low
        return carry

    lax.fori_loop(0, quest_here, body, 0)
    for copy in copies:
        copy.wait()


def own_kernel(query_ref, key_ref, value_ref, probe_ref, stat_ref):
    cont_count, clen, kv_here, head_dim = key_ref.shape
    group = query_ref.shape[2] // kv_here
    cols = clen * group
    chunk = column_chunk(clen, group)
    span = chunk // group
    factor = math.log2(math.e) / math.sqrt(head_dim)
    row = lax.broadcasted_iota(jnp.int32, (span, chunk), 0)
    col = lax.broadcasted_iota(jnp.int32, (span, chunk), 1)
    seen = row * group <= col

    def body(c, carry):
        all_keys, all_values = split_heads(key_ref[c]), split_heads(value_ref[c])
        for k in range(kv_here):
            keys = all_keys[k]
            probe = probe_ref[k * group : (k + 1) * group, :]
            read = dot_nt(all_values[k], jnp.concatenate([probe] * (chunk // group), axis=0))
            for start in range(0, cols, chunk):
                first = start // group
                last = first + span
                query = query_ref[c, first:last, k * group : (k + 1) * group, :].reshape(chunk, head_dim)
                scores = dot_nt(keys[:last], query)
                edge = jnp.where(seen, scores[first:last], -jnp.inf)
                scores = edge if first == 0 else jnp.concatenate([scores[:first], edge], axis=0)
                top = jnp.max(scores, axis=0, keepdims=True)
                expo = jnp.exp2((scores - top) * factor)
                total = jnp.sum(expo, axis=0, keepdims=True)
                summed = jnp.sum(expo * read[:last], axis=0, keepdims=True)
                stat_ref[c, 3 * k : 3 * k + 1, start : start + chunk] = top
                stat_ref[c, 3 * k + 1 : 3 * k + 2, start : start + chunk] = total
                stat_ref[c, 3 * k + 2 : 3 * k + 3, start : start + chunk] = summed
        return carry

    lax.fori_loop(0, cont_count, body, 0)


def prefix_kernel(question_ref, slot_ref, length_ref, query_ref, stat_ref, *rest, wide, quest_here):
    piece_refs, (out_ref, cache, outcome) = rest[:-3], rest[-3:]
    sources = len(piece_refs)
    cont_count, clen, heads_here, head_dim = query_ref.shape
    kv_here = stat_ref.shape[1] // 3
    group = heads_here // kv_here
    cols = clen * group
    chunk = column_chunk(clen, group)
    span = chunk // group
    pref_len = (cache.shape[0] - 2 * heads_here) // kv_here
    factor = math.log2(math.e) / math.sqrt(head_dim)
    me = lax.axis_index("wide")
    outcome[...] = jnp.zeros(outcome.shape, F32)
    base = kv_here * pref_len
    pick_row = lax.broadcasted_iota(jnp.int32, (heads_here, chunk), 0)
    pick_col = lax.broadcasted_iota(jnp.int32, (heads_here, chunk), 1)
    picks = [
        (pick_row == lax.rem(pick_col, group) + k * group).astype(F32).astype(BF16) for k in range(kv_here)
    ]

    def row_of(c):
        return question_ref[lax.div(slot_ref[c], ANSWERS)]

    def body(c, carry):
        wanted = row_of(c)
        if sources == 1:
            pltpu.sync_copy(piece_refs[0].at[wanted], cache)
        else:
            source = lax.rem(me - lax.div(wanted, quest_here) + wide, wide)
            for s in range(sources):

                @pl.when(source == s)
                def _():
                    cache[...] = piece_refs[s][lax.rem(wanted, quest_here)]

        parts = [None] * (cols // chunk)
        for k in range(kv_here):
            keys = cache[k * pref_len : (k + 1) * pref_len, :]
            read = dot_tn(cache[base : base + heads_here, :], picks[k]) + dot_tn(
                cache[base + heads_here : base + 2 * heads_here, :], picks[k]
            )
            for n in range(cols // chunk):
                start = n * chunk
                first = start // group
                query = query_ref[c, first : first + span, k * group : (k + 1) * group, :].reshape(chunk, head_dim)
                scores = dot_nt(keys, query)
                own_top = stat_ref[c, 3 * k : 3 * k + 1, start : start + chunk]
                own_total = stat_ref[c, 3 * k + 1 : 3 * k + 2, start : start + chunk]
                own_sum = stat_ref[c, 3 * k + 2 : 3 * k + 3, start : start + chunk]
                top = jnp.maximum(jnp.max(scores, axis=0, keepdims=True), own_top)
                expo = jnp.exp2((scores - top) * factor)
                shrink = jnp.exp2((own_top - top) * factor)
                total = jnp.sum(expo, axis=0, keepdims=True) + own_total * shrink
                summed = jnp.sum(expo * read, axis=0, keepdims=True) + own_sum * shrink
                value = summed / total
                parts[n] = value if parts[n] is None else parts[n] + value
        for n in range(cols // chunk):
            outcome[pl.ds(c, 1), n * chunk : (n + 1) * chunk] = parts[n]
        return carry

    lax.fori_loop(0, cont_count, body, 0)
    values = outcome[...]
    where_row = lax.broadcasted_iota(jnp.int32, (cols, clen), 0)
    where_col = lax.broadcasted_iota(jnp.int32, (cols, clen), 1)
    fold = (lax.div(where_row, group) == where_col).astype(F32).astype(BF16)
    high = values.astype(BF16).astype(F32)
    middle = (values - high).astype(BF16).astype(F32)
    low = values - high - middle
    stacked = jnp.concatenate([high, middle, low], axis=0).astype(BF16)
    folded = lax.dot_general(stacked, fold, (((1,), (0,)), ((), ())), preferred_element_type=F32)
    rows = outcome.shape[0]
    token = folded[:rows] + folded[rows : 2 * rows] + folded[2 * rows :]
    out_ref[0:rows, :] = token
    lane = lax.broadcasted_iota(jnp.int32, (1, clen), 1)
    spot = spots(out_ref.shape[0] - rows, clen)
    term = jnp.zeros(spot.shape, F32)
    for i in range(cont_count):
        kept = jnp.where(lane < length_ref[i], token[i : i + 1], 0.0)
        choice = jnp.sum(kept, axis=1, keepdims=True)
        target = row_of(i) * ANSWERS + lax.rem(slot_ref[i], ANSWERS)
        term = term + jnp.where(spot == target, choice, 0.0)
    out_ref[rows:, :] = term


def spots(rows, width):
    return lax.broadcasted_iota(jnp.int32, (rows, width), 0) * width + lax.broadcasted_iota(
        jnp.int32, (rows, width), 1
    )


def final_kernel(question_ref, gold_ref, mine_ref, other_ref, near_ref, far_ref, token_ref, logprob_ref, loss_ref):
    cont_count = token_ref.shape[0]
    token_ref[...] = mine_ref[:cont_count, :] + other_ref[:cont_count, :]
    totals = near_ref[...] + far_ref[...]
    quest_here = logprob_ref.shape[0]
    first_row = lax.axis_index("wide") * quest_here
    spot = spots(*totals.shape)
    column = lax.broadcasted_iota(jnp.int32, (1, ANSWERS), 1)

    def total_of(x):
        return jnp.sum(jnp.sum(x, axis=0, keepdims=True), axis=1, keepdims=True)

    for r in range(quest_here):
        row = first_row + r
        shown = (spot >= row * ANSWERS) & (spot < (row + 1) * ANSWERS)
        scores = jnp.where(shown, totals, -jnp.inf)
        top = jnp.max(jnp.max(scores, axis=0, keepdims=True), axis=1, keepdims=True)
        logs = jnp.where(shown, totals - (top + jnp.log(total_of(jnp.exp(scores - top)))), 0.0)
        gold = jnp.int32(0)
        for q in range(question_ref.shape[0]):
            gold = gold + jnp.where(question_ref[q] == row, gold_ref[q], 0)
        line = jnp.zeros((1, ANSWERS), F32)
        for a in range(ANSWERS):
            line = line + jnp.where(column == a, total_of(jnp.where(spot == row * ANSWERS + a, logs, 0.0)), 0.0)
        logprob_ref[r : r + 1, :] = line
        loss_ref[r] = -jnp.sum(jnp.where(spot == row * ANSWERS + gold, logs, 0.0))


def shift(x, axis, by, size):
    return lax.ppermute(x, axis, [(i, (i + by) % size) for i in range(size)])


def swap(x, bit_wide, bit_narrow, wide, narrow):
    pairs = [
        (w * narrow + n, (w ^ bit_wide) * narrow + (n ^ bit_narrow)) for w in range(wide) for n in range(narrow)
    ]
    return lax.ppermute(x, ("wide", "narrow"), pairs)


def in_hbm(x):
    return pltpu.with_memory_space_constraint(x, pltpu.HBM)


def in_vmem(x):
    return pltpu.with_memory_space_constraint(x, pltpu.VMEM)


def per_device(mesh_shape, *args):
    (cont_queries, cont_keys, cont_values, prefix_kv, probe, question_row, cont_slot, cont_length, gold) = args
    wide, narrow = mesh_shape["wide"], mesh_shape["narrow"]
    cont_count, clen, heads_here, head_dim = cont_queries.shape
    kv_here = cont_keys.shape[2]
    group = heads_here // kv_here
    cols = clen * group
    quest_here, _, pref_len = prefix_kv.shape[:3]
    questions = question_row.shape[0]
    packed_rows = kv_here * pref_len + 2 * heads_here

    whole = pl.BlockSpec(memory_space=pltpu.VMEM)
    scalars = pl.BlockSpec(memory_space=pltpu.SMEM)
    outside = pl.BlockSpec(memory_space=pltpu.HBM)
    moved = [in_hbm(x) for x in (cont_queries, cont_keys, cont_values)]
    packed, queries, keys, values = pl.pallas_call(
        pack_kernel,
        in_specs=[whole] * 2 + [outside] * len(moved),
        out_specs=(whole,) * (1 + len(moved)),
        out_shape=(
            jax.ShapeDtypeStruct((quest_here, packed_rows, head_dim), BF16),
            *[pltpu.VMEM(x.shape, x.dtype) for x in moved],
        ),
        scratch_shapes=[pltpu.SemaphoreType.DMA((len(moved),))],
        compiler_params=pltpu.CompilerParams(vmem_limit_bytes=KERNEL_BYTES),
        name="pack",
    )(in_hbm(prefix_kv), in_hbm(probe), *moved)

    if wide <= DIRECT_LIMIT:
        pieces = [packed] + [shift(packed, "wide", by, wide) for by in range(1, wide)]
    else:
        pieces = [lax.all_gather(packed, "wide", axis=0, tiled=True)]
    direct = len(pieces) > 1

    queries = in_vmem(queries)
    stats = pl.pallas_call(
        own_kernel,
        in_specs=[whole] * 4,
        out_specs=whole,
        out_shape=pltpu.VMEM((cont_count, 3 * kv_here, cols), F32),
        cost_estimate=pl.CostEstimate(flops=10**9, bytes_accessed=3 * 10**6, transcendentals=10**6),
        compiler_params=pltpu.CompilerParams(vmem_limit_bytes=KERNEL_BYTES),
        name="own",
    )(queries, in_vmem(keys), in_vmem(values), in_hbm(probe))

    spot_rows = 8 * -(-questions * ANSWERS // (8 * clen))
    rows = 8 * -(-cont_count // 8)
    payload = pl.pallas_call(
        lambda *refs: prefix_kernel(*refs, wide=wide, quest_here=quest_here),
        in_specs=[scalars] * 3 + [whole] * 2 + [whole if direct else outside] * len(pieces),
        out_specs=whole,
        scratch_shapes=[pltpu.VMEM((packed_rows, head_dim), BF16), pltpu.VMEM((rows, cols), F32)],
        out_shape=pltpu.VMEM((rows + spot_rows, clen), F32),
        compiler_params=pltpu.CompilerParams(vmem_limit_bytes=KERNEL_BYTES),
        name="prefix",
    )(question_row, cont_slot, cont_length, in_vmem(queries), in_vmem(stats), *([in_vmem(x) for x in pieces] if direct else pieces))

    mine = payload
    bit = 1
    while 2 * bit < narrow:
        mine = mine + swap(mine, 0, bit, wide, narrow)
        bit *= 2
    other = swap(mine, 0, bit, wide, narrow)
    beside = swap(mine[rows:], 1, 0, wide, narrow)
    across = swap(mine[rows:], 1, bit, wide, narrow)
    near = mine[rows:] + other[rows:] + (beside + across)
    far = jnp.zeros_like(near)
    bit = 2
    while bit < wide:
        near = near + far
        far = swap(near, bit, 0, wide, narrow)
        bit *= 2
    token_score, logprob, owned_loss = pl.pallas_call(
        final_kernel,
        in_specs=[scalars] * 2 + [whole] * 4,
        out_specs=(whole, whole, scalars),
        out_shape=(
            jax.ShapeDtypeStruct((cont_count, clen), F32),
            jax.ShapeDtypeStruct((quest_here, ANSWERS), F32),
            jax.ShapeDtypeStruct((quest_here,), F32),
        ),
        compiler_params=pltpu.CompilerParams(vmem_limit_bytes=KERNEL_BYTES),
        name="final",
    )(question_row, gold, in_vmem(mine), in_vmem(other), in_vmem(near), in_vmem(far))
    return (token_score, logprob, owned_loss)


def solution(mesh):
    shape = dict(mesh.shape)
    if any(size < 2 or size & (size - 1) for size in (shape["wide"], shape["narrow"])):
        raise ValueError("axis size")
    return jax.shard_map(
        lambda *args: per_device(shape, *args),
        mesh=mesh,
        in_specs=(
            P(("groups", "wide"), None, "narrow", None),
            P(("groups", "wide"), None, "narrow", None),
            P(("groups", "wide"), None, "narrow", None),
            P(("groups", "wide"), None, None, "narrow", None),
            P("narrow", None),
            P("groups"),
            P(("groups", "wide")),
            P(("groups", "wide")),
            P("groups"),
        ),
        out_specs=(P(("groups", "wide"), None), P(("groups", "wide"), None), P(("groups", "wide"))),
        check_vma=False,
    )
```

time: 57.8 us -> 32 us (0.55)
  blocking collectives: 35.5 us -> 0 us
  starting transfers between devices: 0 us -> 12 us
  Pallas kernels: 0 us -> 9.98 us
  waiting for transfers between devices: 0 us -> 9.05 us
  other arithmetic: 7.63 us -> 0.01 us
  local copies, waits for them, and re-layouts: 5.13 us -> 0.03 us
  matrix products: 4.82 us -> 0 us
  between operations: 4.47 us -> 0.71 us
    psum x2 -> x0, blocking collectives: 18.1 us -> none  [the longest x1 12.5 us: per_device(): totals = lax.psum(term, 'wide')]
    all_gather x1 -> x0, blocking collectives: 17.4 us -> none  [per_device(): piece = lax.all_gather(prefix_kv, 'wide', axis=0, tiled=True)]
    ppermute x0 -> x8, starting transfers between devices: none -> 12 us  [the longest x3 6.14 us: shift(): return lax.ppermute(x, axis, [(i, (i + by) % size) for i in range(size)])]
    pallas_call x0 -> x4, Pallas kernels: none -> 9.98 us  [the longest x1 3.04 us: per_device(): pl.pallas_call(lambda *refs: prefix_kernel(*refs, wide=wide, quest_here=q...]
    ppermute x0 -> x8, waiting for transfers between devices: none -> 9.05 us  [the longest x5 6.04 us: swap(): return lax.ppermute(x, ('wide', 'narrow'), pairs)]
    reduce_sum x6 -> x0, other arithmetic: 5.49 us -> none  [the longest x1 2.23 us: attend_part(): total = jnp.sum(expo, axis=-1)]
    dot_general x4 -> x0, matrix products: 4.82 us -> none  [the longest x1 2.35 us: attend_part(): jnp.einsum('ckgtj,cjkd->ctkgd', weights, values, preferred_element_type=j...]
    unnamed x17 -> x8, local copies, waits for them, and re-layouts: 3.56 us -> 0.03 us
  transfers between devices with their start and end apart: 0 -> 8, of which waited for: 0 -> 5; matrix products, arithmetic and copies ran while one was open for 0% -> 0% of each run, Pallas kernels for 0% -> 9%
where the time goes in v2:
time: 32 us; the launch traced here: 31.8 us
  starting transfers between devices  12 us (38%)
  Pallas kernels  9.98 us (31%)
  waiting for transfers between devices  9.05 us (28%)
  between operations  0.71 us (2%)
    ppermute x3, starting transfers between devices, shift(): return lax.ppermute(x, axis, [(i, (i + by) % size) for i in range(size)])  6.14 us
    ppermute x5, waiting for transfers between devices, swap(): return lax.ppermute(x, ('wide', 'narrow'), pairs)  6.04 us
    ppermute x5, starting transfers between devices, swap(): return lax.ppermute(x, ('wide', 'narrow'), pairs)  5.85 us
    pallas_call x1, Pallas kernels, per_device(): pl.pallas_call(lambda *refs: prefix_kernel(*refs, wide=wide, quest_here=q...  3.04 us
    ppermute x3, waiting for transfers between devices, shift(): return lax.ppermute(x, axis, [(i, (i + by) % size) for i in range(size)])  3.01 us
    pallas_call x1, Pallas kernels, per_device(): pl.pallas_call(own_kernel, in_specs=[whole] * 4, out_specs=whole, out_sha...  2.95 us
    pallas_call x1, Pallas kernels, per_device(): pl.pallas_call(pack_kernel, in_specs=[whole] * 2 + [outside] * len(moved)...  2.61 us
    pallas_call x1, Pallas kernels, per_device(): pl.pallas_call(final_kernel, in_specs=[scalars] * 2 + [whole] * 4, out_sp...  1.37 us
  transfers between devices with their start and end apart: 8, of which 5 were waited for; matrix products, arithmetic and copies ran while one was open for 0% of the time, Pallas kernels for 9%

profile of v2, /device:TPU:0, one launch (start us, length us, event | category | flops | bytes accessed | tf_op | source)
XLA Modules:
  0.0 31.8 jit_solution(12016433290593514349)
XLA Ops:
  0.6 2.6 %pack.1 = (bf16[1,288,128]{2,1,0:T(8,128)(2,1)S(1)}, bf16[4,128,16,128]{3,2,1,0:T(8,128)(2,1)S(1)}, bf16[4,128,2,128]{3,2,1,0:T(2,128)(2,1)S(1)}, bf16[4,128,2,128]{3,2,1,0:T(2,128)(2,1)S(1)}) custom-call(bf16[1,2,128,2,128]{4,3,2,1,0:T(2,128)(2,1)} %prefix_ref.1, bf16[16,128]{1,0:T(8,128)(2,1)} %probe_ref.3, bf16[4,128,16,128]{3,2,1,0:T(8,128)(2,1)} %refs_0_.2, ...), custom_call_target="tpu_custom_call" | custom-call | tf_op jit(solution)/shard_map/pack/pallas_call | solution.py:263
  3.2 0.0 copy-start
  3.3 0.0 copy-start.1
  3.3 0.0 copy-start.2
  3.3 5.1 %collective-permute-start.2 = (bf16[1,288,128]{2,1,0:T(8,128)(2,1)S(1)}, bf16[1,288,128]{2,1,0:T(8,128)(2,1)S(1)}, u32[]{:S(2)}, u32[]{:S(2)}) collective-permute-start(bf16[1,288,128]{2,1,0:T(8,128)(2,1)S(1)} %get-tuple-element.10.refs_5_), channel_id=1, source_target_pairs={{0,12},{4,0},{8,4},{12,8},{1,13},{5,1},{9,5},{13,9},{2,14},{6,2},{... | collective-permute-start | bytes 221192 | tf_op jit(solution)/shard_map/ppermute | solution.py:230
  8.4 0.0 collective-permute-start.1
  8.4 1.0 %collective-permute-start = (bf16[1,288,128]{2,1,0:T(8,128)(2,1)S(1)}, bf16[1,288,128]{2,1,0:T(8,128)(2,1)S(1)}, u32[]{:S(2)}, u32[]{:S(2)}) collective-permute-start(bf16[1,288,128]{2,1,0:T(8,128)(2,1)S(1)} %get-tuple-element.10.refs_5_), channel_id=1, source_target_pairs={{0,4},{4,8},{8,12},{12,0},{1,5},{5,9},{9,13},{13,1},{2,6},{6,10},{... | collective-permute-start | bytes 221192 | tf_op jit(solution)/shard_map/ppermute | solution.py:230
  9.4 3.0 %own.1.refs_4_ = f32[4,6,1024]{2,1,0:T(8,128)S(1)} custom-call(bf16[4,128,16,128]{3,2,1,0:T(8,128)(2,1)S(1)} %get-tuple-element.7.query_ref.refs_3_, bf16[4,128,2,128]{3,2,1,0:T(2,128)(2,1)S(1)} %get-tuple-element.8.key_ref, bf16[4,128,2,128]{3,2,1,0:T(2,128)(2,1)S(1)} %get-tuple-element.9.value_ref, bf16[16,128]{1,0:T(8,128)(2,1)} %probe_ref.3), custom_call_target="tpu_custom_call" | custom-call | flops 1000000000 | bytes 3000000 | tf_op jit(solution)/shard_map/own/pallas_call | solution.py:283
  12.4 0.0 copy-start.3
  12.4 0.0 collective-permute-done.2.refs_8_
  12.4 3.0 %collective-permute-done.1.refs_7_ = bf16[1,288,128]{2,1,0:T(8,128)(2,1)S(1)} collective-permute-done((bf16[1,288,128]{2,1,0:T(8,128)(2,1)S(1)}, bf16[1,288,128]{2,1,0:T(8,128)(2,1)S(1)}, u32[]{:S(2)}, u32[]{:S(2)}) %collective-permute-start.1) | collective-permute-done | bytes 73760 | tf_op jit(solution)/shard_map/ppermute | solution.py:230
  15.4 0.0 collective-permute-done.refs_6_
  15.4 0.0 copy-done
  15.4 0.0 copy-done.1
  15.4 0.0 copy-done.2
  15.4 3.0 %prefix.1 = f32[16,128]{1,0:T(8,128)S(1)} custom-call(s32[4]{0:T(128)S(1)} %copy-done, s32[4]{0:T(128)S(1)} %copy-done.1, s32[4]{0:T(128)S(1)} %copy-done.2, bf16[4,128,16,128]{3,2,1,0:T(8,128)(2,1)S(1)} %get-tuple-element.7.query_ref.refs_3_, f32[4,6,1024]{2,1,0:T(8,128)S(1)} %own.1.refs_4_, bf16[1,288,128]{2,1,0:T(8,128)(2,1)S(1)} %get-tuple-element.10.refs_5_, ...), custom_call_target="tpu_custom_call" | custom-call | tf_op jit(solution)/shard_map/prefix/pallas_call | solution.py:295
  18.5 0.0 collective-permute-start.3
  18.5 1.2 %collective-permute-done.3 = f32[16,128]{1,0:T(8,128)S(1)} collective-permute-done((f32[16,128]{1,0:T(8,128)S(1)}, f32[16,128]{1,0:T(8,128)S(1)}, u32[]{:S(2)}, u32[]{:S(2)}) %collective-permute-start.3) | collective-permute-done | bytes 8224 | tf_op jit(solution)/shard_map/ppermute | solution.py:237
  19.7 1.5 %collective-permute-start.4 = (f32[16,128]{1,0:T(8,128)S(1)}, f32[16,128]{1,0:T(8,128)S(1)}, u32[]{:S(2)}, u32[]{:S(2)}) collective-permute-start(f32[16,128]{1,0:T(8,128)S(1)} %add.12.mine_ref), channel_id=1, source_target_pairs={{0,2},{1,3},{2,0},{3,1},{4,6},{5,7},{6,4},{7,5},{8,10},{9,11},{10,... | collective-permute-start | bytes 24584 | tf_op jit(solution)/shard_map/ppermute | solution.py:237
  21.1 0.2 collective-permute-start.5
  21.4 1.8 %collective-permute-start.6 = (f32[8,128]{1,0:T(8,128)S(1)}, f32[8,128]{1,0:T(8,128)S(1)}, u32[]{:S(2)}, u32[]{:S(2)}) collective-permute-start(f32[8,128]{1,0:T(8,128)S(1)} %slice.10), channel_id=1, source_target_pairs={{0,6},{1,7},{2,4},{3,5},{4,2},{5,3},{6,0},{7,1},{8,14},{9,15},{10,... | collective-permute-start | bytes 12296 | tf_op jit(solution)/shard_map/ppermute | solution.py:237
  23.2 1.6 %collective-permute-done.5 = f32[8,128]{1,0:T(8,128)S(1)} collective-permute-done((f32[8,128]{1,0:T(8,128)S(1)}, f32[8,128]{1,0:T(8,128)S(1)}, u32[]{:S(2)}, u32[]{:S(2)}) %collective-permute-start.5) | collective-permute-done | bytes 4128 | tf_op jit(solution)/shard_map/ppermute | solution.py:237
  24.8 1.1 %collective-permute-done.6 = f32[8,128]{1,0:T(8,128)S(1)} collective-permute-done((f32[8,128]{1,0:T(8,128)S(1)}, f32[8,128]{1,0:T(8,128)S(1)}, u32[]{:S(2)}, u32[]{:S(2)}) %collective-permute-start.6) | collective-permute-done | bytes 4128 | tf_op jit(solution)/shard_map/ppermute | solution.py:237
  25.9 0.0 collective-permute-done.4.other_ref
  25.9 2.4 %collective-permute-start.7 = (f32[8,128]{1,0:T(8,128)S(1)}, f32[8,128]{1,0:T(8,128)S(1)}, u32[]{:S(2)}, u32[]{:S(2)}) collective-permute-start(f32[8,128]{1,0:T(8,128)S(1)} %fusion.near_ref), channel_id=1, source_target_pairs={{0,8},{1,9},{2,10},{3,11},{4,12},{5,13},{6,14},{7,15},{8,0},{9,1},... | collective-permute-start | bytes 12296 | tf_op jit(solution)/shard_map/ppermute | solution.py:237
  28.2 2.2 %collective-permute-done.7.far_ref = f32[8,128]{1,0:T(8,128)S(1)} collective-permute-done((f32[8,128]{1,0:T(8,128)S(1)}, f32[8,128]{1,0:T(8,128)S(1)}, u32[]{:S(2)}, u32[]{:S(2)}) %collective-permute-start.7) | collective-permute-done | bytes 4128 | tf_op jit(solution)/shard_map/ppermute | solution.py:237
  30.4 0.0 copy-done.3
  30.4 1.4 %final.1 = (f32[4,128]{1,0:T(4,128)}, f32[1,4]{1,0:T(1,128)}, f32[1]{0:T(128)}) custom-call(s32[4]{0:T(128)S(1)} %copy-done, s32[4]{0:T(128)S(1)} %copy-done.3, f32[16,128]{1,0:T(8,128)S(1)} %add.12.mine_ref, f32[16,128]{1,0:T(8,128)S(1)} %collective-permute-done.4.other_ref, f32[8,128]{1,0:T(8,128)S(1)} %fusion.near_ref, ...), custom_call_target="tpu_custom_call" | custom-call | tf_op jit(solution)/shard_map/final/pallas_call | solution.py:320
  (3 shorter events, 0.0 us)
Async XLA Ops:
  3.2 12.2 %copy-start = (s32[4]{0:T(128)S(1)}, s32[4]{0:T(128)}, u32[]{:S(2)}) copy-start(s32[4]{0:T(128)} %question_ref.1) | copy-start | bytes 52
  3.3 12.2 %copy-start.1 = (s32[4]{0:T(128)S(1)}, s32[4]{0:T(128)}, u32[]{:S(2)}) copy-start(s32[4]{0:T(128)} %refs_1_.3) | copy-start | bytes 52
  3.3 12.2 %copy-start.2 = (s32[4]{0:T(128)S(1)}, s32[4]{0:T(128)}, u32[]{:S(2)}) copy-start(s32[4]{0:T(128)} %refs_2_.3) | copy-start | bytes 52
  3.3 9.1 %collective-permute-start.2 = (bf16[1,288,128]{2,1,0:T(8,128)(2,1)S(1)}, bf16[1,288,128]{2,1,0:T(8,128)(2,1)S(1)}, u32[]{:S(2)}, u32[]{:S(2)}) collective-permute-start(bf16[1,288,128]{2,1,0:T(8,128)(2,1)S(1)} %get-tuple-element.10.refs_5_), channel_id=1, source_target_pairs={{0,12},{4,0},{8,4},{12,8},{1,13},{5,1},{9,5},{13,9},{2,14},{6,2},{... | collective-permute-start | bytes 221192 | tf_op jit(solution)/shard_map/ppermute | solution.py:230
  8.4 7.0 %collective-permute-start.1 = (bf16[1,288,128]{2,1,0:T(8,128)(2,1)S(1)}, bf16[1,288,128]{2,1,0:T(8,128)(2,1)S(1)}, u32[]{:S(2)}, u32[]{:S(2)}) collective-permute-start(bf16[1,288,128]{2,1,0:T(8,128)(2,1)S(1)} %get-tuple-element.10.refs_5_), channel_id=1, source_target_pairs={{0,8},{4,12},{8,0},{12,4},{1,9},{5,13},{9,1},{13,5},{2,10},{6,14},... | collective-permute-start | bytes 221192 | tf_op jit(solution)/shard_map/ppermute | solution.py:230
  8.4 7.0 %collective-permute-start = (bf16[1,288,128]{2,1,0:T(8,128)(2,1)S(1)}, bf16[1,288,128]{2,1,0:T(8,128)(2,1)S(1)}, u32[]{:S(2)}, u32[]{:S(2)}) collective-permute-start(bf16[1,288,128]{2,1,0:T(8,128)(2,1)S(1)} %get-tuple-element.10.refs_5_), channel_id=1, source_target_pairs={{0,4},{4,8},{8,12},{12,0},{1,5},{5,9},{9,13},{13,1},{2,6},{6,10},{... | collective-permute-start | bytes 221192 | tf_op jit(solution)/shard_map/ppermute | solution.py:230
  12.4 18.0 %copy-start.3 = (s32[4]{0:T(128)S(1)}, s32[4]{0:T(128)}, u32[]{:S(2)}) copy-start(s32[4]{0:T(128)} %gold_ref.1) | copy-start | bytes 52
  18.5 1.2 %collective-permute-start.3 = (f32[16,128]{1,0:T(8,128)S(1)}, f32[16,128]{1,0:T(8,128)S(1)}, u32[]{:S(2)}, u32[]{:S(2)}) collective-permute-start(f32[16,128]{1,0:T(8,128)S(1)} %prefix.1), channel_id=1, source_target_pairs={{0,1},{1,0},{2,3},{3,2},{4,5},{5,4},{6,7},{7,6},{8,9},{9,8},{10,11... | collective-permute-start | bytes 24584 | tf_op jit(solution)/shard_map/ppermute | solution.py:237
  19.7 6.2 %collective-permute-start.4 = (f32[16,128]{1,0:T(8,128)S(1)}, f32[16,128]{1,0:T(8,128)S(1)}, u32[]{:S(2)}, u32[]{:S(2)}) collective-permute-start(f32[16,128]{1,0:T(8,128)S(1)} %add.12.mine_ref), channel_id=1, source_target_pairs={{0,2},{1,3},{2,0},{3,1},{4,6},{5,7},{6,4},{7,5},{8,10},{9,11},{10,... | collective-permute-start | bytes 24584 | tf_op jit(solution)/shard_map/ppermute | solution.py:237
  21.1 3.6 %collective-permute-start.5 = (f32[8,128]{1,0:T(8,128)S(1)}, f32[8,128]{1,0:T(8,128)S(1)}, u32[]{:S(2)}, u32[]{:S(2)}) collective-permute-start(f32[8,128]{1,0:T(8,128)S(1)} %slice.10), channel_id=1, source_target_pairs={{0,4},{1,5},{2,6},{3,7},{4,0},{5,1},{6,2},{7,3},{8,12},{9,13},{10,... | collective-permute-start | bytes 12296 | tf_op jit(solution)/shard_map/ppermute | solution.py:237
  21.4 4.5 %collective-permute-start.6 = (f32[8,128]{1,0:T(8,128)S(1)}, f32[8,128]{1,0:T(8,128)S(1)}, u32[]{:S(2)}, u32[]{:S(2)}) collective-permute-start(f32[8,128]{1,0:T(8,128)S(1)} %slice.10), channel_id=1, source_target_pairs={{0,6},{1,7},{2,4},{3,5},{4,2},{5,3},{6,0},{7,1},{8,14},{9,15},{10,... | collective-permute-start | bytes 12296 | tf_op jit(solution)/shard_map/ppermute | solution.py:237
  25.9 4.5 %collective-permute-start.7 = (f32[8,128]{1,0:T(8,128)S(1)}, f32[8,128]{1,0:T(8,128)S(1)}, u32[]{:S(2)}, u32[]{:S(2)}) collective-permute-start(f32[8,128]{1,0:T(8,128)S(1)} %fusion.near_ref), channel_id=1, source_target_pairs={{0,8},{1,9},{2,10},{3,11},{4,12},{5,13},{6,14},{7,15},{8,0},{9,1},... | collective-permute-start | bytes 12296 | tf_op jit(solution)/shard_map/ppermute | solution.py:237
